TPU v7x, 32 devices: a whole 2x2x4 slice. The times are simulated.
32 devices in a mesh: gx: 8 (over y, x, core), gy: 4 (over z).
Axes of the slice: x: 2, y: 2, z: 4, core: 2. Of those that a mesh axis runs over, the one named last changes fastest.
Arguments:
- sky_interface_transfers: bfloat16 [4, 384, 1024], P(None, 'gy', 'gx'), may hold values from -6 to 6
- coupling_matrix_enlarged: bfloat16 [384, 1024, 128], P('gy', 'gx'), may hold values from -0.5 to 0.5
- piece_keeper_part: int32 [8, 384, 1], P('gx', 'gy'), may hold values from 0 to 31; in each aligned block of 96 rows (0 to 95, 96 to 191, ..., all dimensions but the last counted through in order) at most 6 rows name the same one
- receiving_part_line: int32 [8, 384], P('gx', 'gy'), may hold values from 0 to 127
- marine_point_switch: int32 [1024, 512], P('gx', 'gy'), may hold values 0 or 1
- potential_heat_deviation: float32 [8, 1024, 512], P(None, 'gx', 'gy'), may hold values from -6 to 6
- free_marine_lift: float32 [1024, 512], P('gx', 'gy'), may hold values from -3 to 3
- depth_averaged_uflow: float32 [1024, 512], P('gx', 'gy'), may hold values from -3 to 3
- depth_averaged_vflow: float32 [1024, 512], P('gx', 'gy'), may hold values from -3 to 3
Outputs:
- atmo_skin_temp_back: float32 [384, 1024], P('gy', 'gx')
- ocean_temp_after_step: float32 [8, 1024, 512], P(None, 'gx', 'gy')
- barotropic: float32 [3, 1024, 512], P(None, 'gx', 'gy')
Inputs may be any that keep to these rules, and one draw needn't show every extreme that they name: `piece_keeper_part`: ocean devices are counted with gx slowest. Among the 96 blocks of one atmosphere device at most 6 have the same owner, and some device has exactly 6 with one owner; every ocean device owns some block.
All inputs are finite; a program needn't handle non-finite values. No bound on the sum of `marine_point_switch` on one device may be relied on, other than what follows from the above.
Results may differ from a plain program's by a relative error of at most 0.0026.
Values may be sent and summed in bfloat16 or wider, within the bound.
A program may use at most 64 MiB of HBM per device.

v0:
```python
import jax
import jax.numpy as jnp
from jax import lax
from jax.experimental import pallas as pl
from jax.experimental.pallas import tpu as pltpu
from jax.sharding import PartitionSpec as P

NB = 96
OX = 128
BAND_NORTH_COUNT = 128
MARINE_STRATA = 8
SUB = 40


HORIZ_MIX = 0.15
VERT_MIX = 0.2
HEAT_GAIN = 0.5
FLOW_DAMP = 0.98
PRESS_GAIN = 0.6
DIVERGE_GAIN = 0.6
CORIOLIS = 0.1
WIND_GAIN = 0.05
FRESH_GAIN = 0.05


MESH = pl.DeviceIdType.MESH
LANES = BAND_NORTH_COUNT
HALF = LANES // 2
SPAN = SUB // 2
MARGIN = 2 * SPAN
BASE = MARGIN + 8
TALL = OX + 2 * BASE
FRAME = OX + 2 * MARGIN
OVERLAP = (LANES - 2 * MARGIN) // 2
GROUP = 4
RENEW = 3 * GROUP
CHUNK = 16
SLOTS = 8
FLUXES = 4
PARTS = 4


def turn_lanes(values, shift):
    shift = shift % LANES
    return pltpu.roll(values, shift, 1) if shift else values


def lanes(rows):
    return lax.broadcasted_iota(jnp.int32, (rows, LANES), 1)


def neighbours():
    nx, ny = lax.axis_size("gx"), lax.axis_size("gy")
    x, y = lax.axis_index("gx"), lax.axis_index("gy")
    up, down = lax.rem(x + 1, nx), lax.rem(x + nx - 1, nx)
    right, left = lax.rem(y + 1, ny), lax.rem(y + ny - 1, ny)
    return x, y, up, down, right, left


def peer_place(index):
    ny = lax.axis_size("gy")
    return lax.div(index, ny), lax.rem(index, ny)


def greet_all(me, count):
    barrier = pltpu.get_barrier_semaphore()

    def one(k, carry):
        place = peer_place(lax.rem(me + k, count))
        pl.semaphore_signal(barrier, inc=1, device_id=place, device_id_type=MESH)
        return carry

    lax.fori_loop(1, count, one, 0)


def peers(action, out, into, send_sem, recv_sem):
    nx, ny = lax.axis_size("gx"), lax.axis_size("gy")
    x, y = lax.axis_index("gx"), lax.axis_index("gy")
    me = x * ny + y
    for dy in sorted(range(ny), key=lambda d: abs(2 * d - ny)):

        def one(dx, carry, dy=dy):
            to_x, to_y = lax.rem(x + dx, nx), lax.rem(y + dy, ny)
            copy = pltpu.make_async_remote_copy(
                src_ref=out.at[to_x * ny + to_y],
                dst_ref=into.at[me],
                send_sem=send_sem.at[dx * ny + dy],
                recv_sem=recv_sem.at[dx * ny + dy],
                device_id=(to_x, to_y),
                device_id_type=MESH,
            )
            if action == "start":
                copy.start()
            else:
                copy.wait()
            return carry

        lax.fori_loop(0 if dy else 1, nx, one, 0)


def as_bits(condition):
    return jnp.where(condition, 1.0, 0.0).astype(jnp.bfloat16)


def line_numbers(shape, axis):
    return lax.broadcasted_iota(jnp.int32, shape, axis).astype(jnp.float32)


def dot(a, b, a_dim=1, b_dim=0):
    return lax.dot_general(
        a, b, (((a_dim,), (b_dim,)), ((), ())), preferred_element_type=jnp.float32
    )


def place_blocks(keeper, lines, count):
    i, j = line_numbers((NB, NB), 0), line_numbers((NB, NB), 1)
    owner_row = keeper[...].astype(jnp.float32)
    owner_col = jnp.sum(jnp.where(i == j, owner_row, 0.0), axis=1, keepdims=True)
    same = jnp.where(owner_col == owner_row, 1.0, 0.0)
    rank_row = jnp.sum(jnp.where(i < j, same, 0.0), axis=0, keepdims=True)
    rank_col = jnp.sum(jnp.where(j < i, same, 0.0), axis=1, keepdims=True)
    line_row = lines[...].astype(jnp.float32)
    line_col = jnp.sum(jnp.where(i == j, line_row, 0.0), axis=1, keepdims=True)
    owned = as_bits(line_numbers((count, NB), 0) == owner_row)
    ranked = jnp.where(line_numbers((NB, LANES), 1) == rank_col, line_col + 1.0, 0.0)
    listed = dot(owned, ranked.astype(jnp.bfloat16))
    return owner_row * SLOTS + rank_row, owner_col * SLOTS + rank_col, listed


def regrid(sky, weights, partial, waits):
    slot32 = lax.rem(lax.broadcasted_iota(jnp.int32, (FLUXES * SLOTS, LANES), 0), SLOTS)
    groups = NB // SLOTS
    for g in range(groups):
        if g % (groups // PARTS) == 0:
            waits[g // (groups // PARTS)].wait()
        rows = slice(g * SLOTS, (g + 1) * SLOTS)
        fluxes = sky[:, rows, :].astype(jnp.float32).reshape(FLUXES * SLOTS, OX)
        fluxes = fluxes.astype(jnp.bfloat16)
        total = dot(fluxes, weights[g * SLOTS])
        for n in range(1, SLOTS):
            total = jnp.where(slot32 == n, dot(fluxes, weights[g * SLOTS + n]), total)
        partial[:, rows, :] = total.reshape(FLUXES, SLOTS, LANES)


def fill_send(send, stage, partial, slots, count, most):
    rows = FLUXES * most
    pairs = []
    for f in range(0, FLUXES, 2):
        both = jnp.concatenate([partial[f], partial[f + 1]], axis=1).astype(jnp.bfloat16)
        pairs.append(dot(slots, both))
    for d in range(count):
        for f in range(FLUXES):
            at = d * rows + f * most
            from_lane = (f % 2) * LANES
            stage[at : at + SLOTS] = pairs[f // 2][
                d * SLOTS : (d + 1) * SLOTS, from_lane : from_lane + LANES
            ]
    send[...] = stage[0 : count * rows].reshape(count, rows, LANES).astype(jnp.bfloat16)


def read_targets(listed_in, count):
    lane = line_numbers((SLOTS, LANES), 1)
    row = line_numbers((SLOTS, LANES), 0)
    tiles = []
    for s in range(count):
        line = jnp.broadcast_to(listed_in[s], (SLOTS, LANES))
        line = jnp.sum(jnp.where(lane == row, line, 0.0), axis=1, keepdims=True)
        tiles.append(jnp.where(lane + 1.0 == line, 1.0, 0.0))
    return jnp.concatenate(tiles, axis=0)


def read_fluxes(recv, stage, count, most):
    rows = FLUXES * most
    stage[0 : count * rows] = recv[...].astype(jnp.float32).reshape(count * rows, LANES)
    values = []
    for f in range(FLUXES):
        starts = [s * rows + f * most for s in range(count)]
        tiles = [stage[at : at + SLOTS] for at in starts]
        values.append(jnp.concatenate(tiles, axis=0).astype(jnp.bfloat16))
    return values


def edge_selector(rows, low_row, high_row):
    row = lax.broadcasted_iota(jnp.int32, (rows, BAND_NORTH_COUNT), 0)
    lane = lax.broadcasted_iota(jnp.int32, (rows, BAND_NORTH_COUNT), 1)
    return as_bits(
        ((row == low_row) & (lane == 0)) | ((row == high_row) & (lane == BAND_NORTH_COUNT - 1))
    )


def fill_heat_edges(heat, edges):
    selector = edge_selector(8, 0, 1)
    for k in range(MARINE_STRATA):
        level = slice(k, k + 1)
        edges[0, level] = heat[k, 0:1]
        edges[1, level] = heat[k, OX - 1 : OX]
        sides = dot(selector, heat[k].astype(jnp.bfloat16), 1, 1)
        edges[2, level] = sides[0:1]
        edges[3, level] = sides[1:2]


def heat_copies(edges, got, send_sem, recv_sem):
    x, y, up, down, right, left = neighbours()
    plan = ((1, 0, (up, y)), (0, 1, (down, y)), (3, 2, (x, right)), (2, 3, (x, left)))
    return [
        pltpu.make_async_remote_copy(
            src_ref=edges.at[src],
            dst_ref=got.at[dst],
            send_sem=send_sem.at[k],
            recv_sem=recv_sem.at[k],
            device_id=place,
            device_id_type=MESH,
        )
        for k, (src, dst, place) in enumerate(plan)
    ]


def heat_step(heat, got, tall, shore, left_wet, right_wet, near, out):
    last = lanes(OX) == LANES - 1
    first = lanes(OX) == 0
    mine = shore[8 : 8 + OX]
    near[0] = jnp.where(last, turn_lanes(right_wet, -1), turn_lanes(mine, -1))
    near[1] = jnp.where(first, turn_lanes(left_wet, 1), turn_lanes(mine, 1))
    sides = jnp.concatenate([got[3], got[2]], axis=0).astype(jnp.bfloat16)
    for k in range(MARINE_STRATA):
        tall[k, 8 : 8 + OX] = heat[k]
        tall[k, 7:8] = got[0, k : k + 1]
        tall[k, 8 + OX : 9 + OX] = got[1, k : k + 1]
        near[2 + k] = dot(sides, edge_selector(2 * MARINE_STRATA, MARINE_STRATA + k, k), 0, 0)

    step = 32
    last, first = last[:step], first[:step]

    def one(k, carry):
        above, below = jnp.maximum(k - 1, 0), jnp.minimum(k + 1, MARINE_STRATA - 1)
        for start in range(0, OX, step):
            rows = slice(start, start + step)
            tall_rows = lambda shift: slice(8 + start + shift, 8 + start + step + shift)
            here = heat[k, rows]
            side = near[2 + k, rows]
            north = jnp.where(last, side, turn_lanes(here, -1))
            south = jnp.where(first, side, turn_lanes(here, 1))
            lateral = shore[tall_rows(1)] * (tall[k, tall_rows(1)] - here)
            lateral = lateral + shore[tall_rows(-1)] * (tall[k, tall_rows(-1)] - here)
            lateral = lateral + near[0, rows] * (north - here)
            lateral = lateral + near[1, rows] * (south - here)
            vertical = (heat[above, rows] - here) + (heat[below, rows] - here)
            out[k, rows] = (here + HORIZ_MIX * lateral + VERT_MIX * vertical) * shore[tall_rows(0)]
        return carry

    lax.fori_loop(0, MARINE_STRATA, one, 0)


def remote(src, dst, place, send, recv, k):
    return pltpu.make_async_remote_copy(
        src_ref=src,
        dst_ref=dst,
        send_sem=send.at[k],
        recv_sem=recv.at[k],
        device_id=place,
        device_id_type=MESH,
    )


class Exchange:
    def __init__(self, rows, edge, packs, sides, send, recv, wrap):
        x, y, up, down, right, left = neighbours()
        ny = lax.axis_size("gy")
        low, high = packs.at[0], packs.at[1]
        from_left, from_right = sides.at[0], sides.at[1]
        top, whole, bottom = pl.ds(OX - MARGIN, MARGIN), pl.ds(0, OX), pl.ds(0, MARGIN)
        before, middle, after = pl.ds(0, MARGIN), pl.ds(MARGIN, OX), pl.ds(MARGIN + OX, MARGIN)
        moves = ((top, before, up), (bottom, after, down), (whole, middle, x))
        self.rows = []
        if rows is not None:
            self.rows = [
                remote(rows.at[1], edge.at[0], (up, y), send, recv, 6),
                remote(rows.at[0], edge.at[1], (down, y), send, recv, 7),
            ]
        self.right = [
            remote(high.at[src], from_left.at[dst], (to, right), send, recv, k)
            for k, (src, dst, to) in enumerate(moves)
        ]
        self.left = [
            remote(low.at[src], from_right.at[dst], (to, left), send, recv, 3 + k)
            for k, (src, dst, to) in enumerate(moves)
        ]
        self.wrap, self.has_right, self.has_left = wrap, y < ny - 1, y > 0

    def guarded(self, condition, copies, action):
        def act():
            for copy in copies:
                getattr(copy, action)()

        if self.wrap:
            act()
        else:
            pl.when(condition)(act)

    def start(self):
        self.guarded(self.has_right, self.right, "start")
        self.guarded(self.has_left, self.left, "start")
        for copy in self.rows:
            copy.start()

    def wait(self):
        for copy in self.rows:
            copy.wait()
        self.guarded(self.has_left, self.right, "wait_recv")
        self.guarded(self.has_right, self.left, "wait_recv")
        self.guarded(self.has_right, self.right, "wait_send")
        self.guarded(self.has_left, self.left, "wait_send")


def clear_walls(sides):
    y, ny = lax.axis_index("gy"), lax.axis_size("gy")
    blank = jnp.zeros((FRAME, LANES), jnp.bfloat16)

    @pl.when(y == 0)
    def _():
        for side in sides:
            side[0] = blank

    @pl.when(y == ny - 1)
    def _():
        for side in sides:
            side[1] = blank


def fill_rows(rows, field, values):
    rows[0, field] = values[:MARGIN].astype(jnp.bfloat16)
    rows[1, field] = values[OX - MARGIN :].astype(jnp.bfloat16)


def fill_packs(packs, values):
    lane = lanes(OX)
    low = turn_lanes(values[2], LANES - 3 * MARGIN)
    low = jnp.where(lane >= LANES - 2 * MARGIN, turn_lanes(values[1], LANES - 2 * MARGIN), low)
    low = jnp.where(lane >= LANES - MARGIN, turn_lanes(values[0], LANES - MARGIN), low)
    high = turn_lanes(values[2], 3 * MARGIN)
    high = jnp.where(lane < 2 * MARGIN, turn_lanes(values[1], 2 * MARGIN), high)
    high = jnp.where(lane < MARGIN, turn_lanes(values[0], MARGIN), high)
    packs[0] = low.astype(jnp.bfloat16)
    packs[1] = high.astype(jnp.bfloat16)


def zones():
    return (
        (BASE - MARGIN, 0, MARGIN, 0),
        (BASE, MARGIN, OX, None),
        (BASE + OX, MARGIN + OX, MARGIN, 1),
    )


def spread_fields(natural, edge, sides, wide, mask):
    for at, side_at, size, end in zones():
        lane = lanes(size)
        here, there = slice(at, at + size), slice(side_at, side_at + size)
        from_left = sides[0, there].astype(jnp.float32)
        from_right = sides[1, there].astype(jnp.float32)
        for f in range(3):
            centre = natural[f] if end is None else edge[end, f].astype(jnp.float32)
            left = turn_lanes(from_left, -f * MARGIN)
            right = turn_lanes(from_right, f * MARGIN)
            one = jnp.where(lane < MARGIN, left, turn_lanes(centre, MARGIN))
            two = jnp.where(lane >= LANES - MARGIN, right, turn_lanes(centre, -MARGIN))
            if mask is not None and f > 0:
                one = jnp.where(mask[0, here] > 0, one, 0.0)
                two = jnp.where(mask[1, here] > 0, two, 0.0)
            wide[f, 0, here] = one
            wide[f, 1, here] = two


def spread_wet(shore, edge, sides, gain):
    for at, side_at, size, end in zones():
        lane = lanes(size)
        here, there = slice(at, at + size), slice(side_at, side_at + size)
        from_left = sides[0, there].astype(jnp.float32)
        from_right = sides[1, there].astype(jnp.float32)
        centre = shore[8 : 8 + OX] if end is None else edge[end, 3].astype(jnp.float32)
        one = jnp.where(lane >= LANES - MARGIN, from_left, centre)
        two = jnp.where(lane < MARGIN, from_right, centre)
        gain[0, here] = PRESS_GAIN * turn_lanes(one, MARGIN)
        gain[1, here] = PRESS_GAIN * turn_lanes(two, -MARGIN)


def renew_overlap(state, reach):
    low, high = BASE - reach, BASE + OX + reach
    shift = LANES - 2 * MARGIN + 2 * OVERLAP
    for start in range(low, high, CHUNK):
        rows = slice(start, start + CHUNK)
        lane = lanes(CHUNK)
        for f in range(3):
            one, two = state[f, 0, rows], state[f, 1, rows]
            state[f, 0, rows] = jnp.where(lane >= LANES - OVERLAP, turn_lanes(two, 2 * MARGIN), one)
            state[f, 1, rows] = jnp.where(lane < OVERLAP, turn_lanes(one, -2 * MARGIN), two)


def own_part(state, f, rows=None):
    one, two = state[f, 0, BASE : BASE + OX], state[f, 1, BASE : BASE + OX]
    return jnp.where(lanes(OX) < HALF, turn_lanes(one, -MARGIN), turn_lanes(two, MARGIN))


def substep(reach, state, forces, gain, turning, raw):
    low, high = BASE - reach, BASE + OX + reach
    turn = [jnp.broadcast_to(turning[tile : tile + 1, :], (CHUNK, LANES)) for tile in range(2)]

    def velocity(start, tile):
        rows = slice(start, start + CHUNK)
        height = state[0, tile, rows]
        slope_east = (
            state[0, tile, start + 1 : start + CHUNK + 1]
            - state[0, tile, start - 1 : start + CHUNK - 1]
        )
        slope_north = turn_lanes(height, -1) - turn_lanes(height, 1)
        old_u, old_v, slope = state[1, tile, rows], state[2, tile, rows], gain[tile, rows]
        new_u = (FLOW_DAMP * old_u + turn[tile] * old_v) + (
            forces[0, tile, rows] - slope * slope_east
        )
        new_v = (FLOW_DAMP * old_v + (forces[1, tile, rows] - slope * slope_north)) - (
            turn[tile] * new_u
        )
        state[1, tile, rows] = new_u
        state[2, tile, rows] = new_v

    def surface(start, tile):
        rows = slice(start, start + CHUNK)
        flow_north = state[2, tile, rows]
        spread_east = (
            state[1, tile, start + 1 : start + CHUNK + 1]
            - state[1, tile, start - 1 : start + CHUNK - 1]
        )
        spread_north = turn_lanes(flow_north, -1) - turn_lanes(flow_north, 1)
        height, slope = state[0, tile, rows], gain[tile, rows]
        if raw:
            height = jnp.where(slope > 0, height, 0.0)
        state[0, tile, rows] = (height - forces[2, tile, rows]) - slope * (
            spread_east + spread_north
        )

    starts = range(low, high, CHUNK)
    for start in starts:
        for tile in range(2):
            velocity(start, tile)
        if start > low:
            for tile in range(2):
                surface(start - CHUNK, tile)
    for tile in range(2):
        surface(high - CHUNK, tile)


def run_span(state, forces, gain, turning, raw):
    done = 0
    while done < SPAN:
        need = 2 * (SPAN - done) - 1
        reach = -(-need // 8) * 8
        steps = min(SPAN - done, GROUP)
        if done == RENEW:
            renew_overlap(state, reach)
        if raw and done == 0:
            substep(reach, state, forces, gain, turning, True)

        def one(_, carry, reach=reach):
            substep(reach, state, forces, gain, turning, False)
            return carry

        lax.fori_loop(1 if raw and done == 0 else 0, steps, one, 0)
        done += steps


def window_kernel(
    sky_far, weights_far, keeper_far, lines_far, sea_far, heat_far, h_far, u_far, v_far,
    back, heat_out, out,
    sky, weights, keeper, lines, sea, heat, natural,
    turning, partial, stage, send, recv, listed_out, listed_in, skin_send, skin_recv,
    heat_edges, heat_got, tall, near, shore,
    state, forces, gain,
    rows1, edge1, packs1, sides1, wets, wets_in,
    rows2, edge2, packs2, sides2, rows3, edge3, packs3, sides3,
    load_sem, list_send, list_recv, a2a_send, a2a_recv, skin_send_sem, skin_recv_sem,
    heat_send_sem, heat_recv_sem, send0, recv0, send1, recv1, send2, recv2, send3, recv3,
):
    ny = lax.axis_size("gy")
    count = lax.axis_size("gx") * ny
    most = max(2, 2 * NB // count)
    me = lax.axis_index("gx") * ny + lax.axis_index("gy")
    greet_all(me, count)
    part = NB // PARTS
    pieces = [pl.ds(p * part, part) for p in range(PARTS)]
    moves = [(keeper_far, keeper), (lines_far, lines), (sky_far, sky)]
    moves += [(weights_far.at[piece], weights.at[piece]) for piece in pieces]
    moves += [(sea_far, sea), (h_far, natural.at[0]), (u_far, natural.at[1])]
    moves += [(v_far, natural.at[2]), (heat_far, heat)]
    loads = [
        pltpu.make_async_copy(src, dst, load_sem.at[k]) for k, (src, dst) in enumerate(moves)
    ]
    for load in loads:
        load.start()
    turning[...] = turning_rows()
    clear_walls((sides2, sides3, wets_in))
    blank = jnp.zeros((8, LANES), jnp.float32)
    for f in range(2):
        for tile in range(2):
            state[f, tile, BASE - MARGIN - 8 : BASE - MARGIN] = blank
            state[f, tile, BASE + OX + MARGIN : BASE + OX + MARGIN + 8] = blank
    stage[count * FLUXES * most : count * FLUXES * most + SLOTS] = blank
    loads[0].wait()
    loads[1].wait()
    key_row, key_col, listed = place_blocks(keeper, lines, count)
    for d in range(count):
        listed_out[d] = listed[d : d + 1]
    slots = as_bits(line_numbers((count * SLOTS, NB), 0) == key_row)
    loads[2].wait()
    regrid(sky, weights, partial, loads[3 : 3 + PARTS])
    fill_send(send, stage, partial, slots, count, most)
    pl.semaphore_wait(pltpu.get_barrier_semaphore(), count - 1)
    peers("start", listed_out, listed_in, list_send, list_recv)
    peers("start", send, recv, a2a_send, a2a_recv)
    recv[me] = send[me]
    listed_in[me] = listed_out[me]
    for load in loads[3 + PARTS :]:
        load.wait()
    lat = lax.axis_index("gy") * LANES + lanes(OX)
    inside = (lat > 0) & (lat < ny * LANES - 1)
    shore[8 : 8 + OX] = jnp.where(inside, sea[...].astype(jnp.float32), 0.0)
    fill_heat_edges(heat, heat_edges)
    heats = heat_copies(heat_edges, heat_got, heat_send_sem, heat_recv_sem)
    for copy in heats:
        copy.start()
    for f in range(3):
        fill_rows(rows1, f, natural[f])
    fill_rows(rows1, 3, shore[8 : 8 + OX])
    fill_packs(packs1, [natural[f] for f in range(3)])
    wets[0] = shore[8 : 8 + OX].astype(jnp.bfloat16)
    wets[1] = shore[8 : 8 + OX].astype(jnp.bfloat16)
    first = Exchange(rows1, edge1, packs1, sides1, send1, recv1, True)
    wet = Exchange(None, None, wets, wets_in, send0, recv0, False)
    wet.start()
    first.start()
    peers("wait", listed_out, listed_in, list_send, list_recv)
    target = read_targets(listed_in, count)
    target_turned = target.T.astype(jnp.bfloat16)
    target = target.astype(jnp.bfloat16)
    peers("wait", send, recv, a2a_send, a2a_recv)
    values = read_fluxes(recv, stage, count, most)
    stress = dot(target_turned, jnp.concatenate([values[0], values[1]], axis=1))
    others = dot(target_turned, jnp.concatenate([values[3], values[2]], axis=1))
    mask = shore[8 : 8 + OX]
    own = [
        WIND_GAIN * stress[:, :LANES] * mask,
        WIND_GAIN * stress[:, LANES:] * mask,
        FRESH_GAIN * others[:, :LANES] * mask,
    ]
    for f in range(3):
        fill_rows(rows2, f, own[f])
    fill_packs(packs2, own)
    second = Exchange(rows2, edge2, packs2, sides2, send2, recv2, False)
    second.start()
    wet.wait()
    first.wait()
    for copy in heats:
        copy.wait()
    spread_wet(shore, edge1, wets_in, gain)
    spread_fields(natural, edge1, sides1, state, gain)
    shore[7:8] = edge1[0, 3, MARGIN - 8 : MARGIN].astype(jnp.float32)[7:8]
    shore[8 + OX : 9 + OX] = edge1[1, 3, 0:8].astype(jnp.float32)[0:1]
    left_wet = wets_in[0, MARGIN : MARGIN + OX].astype(jnp.float32)
    right_wet = wets_in[1, MARGIN : MARGIN + OX].astype(jnp.float32)
    heat_step(heat, heat_got, tall, shore, left_wet, right_wet, near, heat_out)
    surface = heat_out[0] + HEAT_GAIN * others[:, LANES:] * shore[8 : 8 + OX]
    heat_out[0] = surface
    band = dot(target, surface.astype(jnp.bfloat16))
    skin_send[...] = band.reshape(count, SLOTS, LANES).astype(jnp.bfloat16)
    peers("start", skin_send, skin_recv, skin_send_sem, skin_recv_sem)
    skin_recv[me] = skin_send[me]
    second.wait()
    spread_fields(own, edge2, sides2, forces, None)
    run_span(state, forces, gain, turning, True)
    for f in range(3):
        natural[f] = own_part(state, f)
        fill_rows(rows3, f, natural[f])
    fill_packs(packs3, [natural[f] for f in range(3)])
    third = Exchange(rows3, edge3, packs3, sides3, send3, recv3, False)
    third.start()
    peers("wait", skin_send, skin_recv, skin_send_sem, skin_recv_sem)
    slots = as_bits(line_numbers((NB, count * SLOTS), 1) == key_col)
    skin = dot(slots, skin_recv[...].reshape(count * SLOTS, LANES))
    slot8 = lax.broadcasted_iota(jnp.int32, (SLOTS, LANES), 0)
    for g in range(NB // SLOTS):
        rows = slice(g * SLOTS, (g + 1) * SLOTS)
        lines_skin = skin[rows].astype(jnp.bfloat16)
        total = dot(lines_skin, weights[g * SLOTS], 1, 1)
        for n in range(1, SLOTS):
            total = jnp.where(slot8 == n, dot(lines_skin, weights[g * SLOTS + n], 1, 1), total)
        back[rows] = total
    third.wait()
    spread_fields(natural, edge3, sides3, state, None)
    run_span(state, forces, gain, turning, False)
    for f in range(3):
        out[f] = own_part(state, f)


def turning_rows():
    total_y = lax.axis_size("gy") * LANES
    shape = (8, LANES)
    lane = lax.broadcasted_iota(jnp.int32, shape, 1)
    tile = lax.broadcasted_iota(jnp.int32, shape, 0)
    rows = lax.axis_index("gy") * LANES + lane + jnp.where(tile == 0, -MARGIN, MARGIN)
    rows = jnp.where(rows < 0, rows + total_y, jnp.where(rows < total_y, rows, rows - total_y))
    return CORIOLIS * jnp.sin(jnp.pi * ((rows.astype(jnp.float32) + 0.5) / total_y - 0.5))


def hand_over(*refs):
    sources, targets = refs[:3], refs[3:6]
    buffers, loads, stores = refs[6:9], refs[9], refs[10]
    into = [
        pltpu.make_async_copy(sources[k], buffers[k], loads.at[k]) for k in range(3)
    ]
    away = [
        pltpu.make_async_copy(buffers[k], targets[k], stores.at[k]) for k in range(3)
    ]
    for copy in into:
        copy.start()
    for k in range(3):
        into[k].wait()
        away[k].start()
    for copy in away:
        copy.wait()


def per_device(
    sky_interface_transfers,
    coupling_matrix_enlarged,
    piece_keeper_part,
    receiving_part_line,
    marine_point_switch,
    potential_heat_deviation,
    free_marine_lift,
    depth_averaged_uflow,
    depth_averaged_vflow,
):
    count = lax.axis_size("gx") * lax.axis_size("gy")
    most = max(2, 2 * NB // count)
    line = LANES
    half = jnp.bfloat16
    full = jnp.float32

    def boxes(fields):
        return [
            pltpu.VMEM((2, fields, MARGIN, line), half),
            pltpu.VMEM((2, fields, MARGIN, line), half),
            pltpu.VMEM((2, OX, line), half),
            pltpu.VMEM((2, FRAME, line), half),
        ]

    inside = pl.BlockSpec(memory_space=pltpu.VMEM)
    far = pl.BlockSpec(memory_space=pltpu.HBM)
    shapes = (
        jax.ShapeDtypeStruct((NB, OX), full),
        jax.ShapeDtypeStruct((MARINE_STRATA, OX, line), full),
        jax.ShapeDtypeStruct((3, OX, line), full),
    )
    results = pl.pallas_call(
        window_kernel,
        out_shape=shapes,
        in_specs=[far] * 9,
        out_specs=(inside,) * 3,
        scratch_shapes=[
            pltpu.VMEM((FLUXES, NB, OX), half),
            pltpu.VMEM((NB, OX, line), half),
            pltpu.VMEM((1, NB), jnp.int32),
            pltpu.VMEM((1, NB), jnp.int32),
            pltpu.VMEM((OX, line), jnp.int32),
            pltpu.VMEM((MARINE_STRATA, OX, line), full),
            pltpu.VMEM((3, OX, line), full),
            pltpu.VMEM((8, line), full),
            pltpu.VMEM((FLUXES, NB, line), full),
            pltpu.VMEM((count * FLUXES * most + SLOTS, line), full),
            pltpu.VMEM((count, FLUXES * most, line), half),
            pltpu.VMEM((count, FLUXES * most, line), half),
            pltpu.VMEM((count, 1, line), full),
            pltpu.VMEM((count, 1, line), full),
            pltpu.VMEM((count, SLOTS, line), half),
            pltpu.VMEM((count, SLOTS, line), half),
            pltpu.VMEM((4, MARINE_STRATA, line), full),
            pltpu.VMEM((4, MARINE_STRATA, line), full),
            pltpu.VMEM((MARINE_STRATA, OX + 16, line), full),
            pltpu.VMEM((2 + MARINE_STRATA, OX, line), full),
            pltpu.VMEM((OX + 16, line), full),
            pltpu.VMEM((3, 2, TALL, line), full),
            pltpu.VMEM((3, 2, TALL, line), full),
            pltpu.VMEM((2, TALL, line), full),
        ]
        + boxes(4)
        + [pltpu.VMEM((2, OX, line), half), pltpu.VMEM((2, FRAME, line), half)]
        + boxes(3)
        + boxes(3)
        + [pltpu.SemaphoreType.DMA((3 + PARTS + 5,))]
        + [pltpu.SemaphoreType.DMA((count,))] * 6
        + [pltpu.SemaphoreType.DMA((4,))] * 2
        + [pltpu.SemaphoreType.DMA((8,))] * 8,
        compiler_params=pltpu.CompilerParams(
            collective_id=0, has_side_effects=True, vmem_limit_bytes=24 * 1024 * 1024
        ),
        name="window",
    )(
        *[
            pltpu.with_memory_space_constraint(value, pltpu.HBM)
            for value in (
                sky_interface_transfers,
                coupling_matrix_enlarged,
                piece_keeper_part.reshape(1, NB),
                receiving_part_line,
                marine_point_switch,
                potential_heat_deviation,
                free_marine_lift,
                depth_averaged_uflow,
                depth_averaged_vflow,
            )
        ]
    )
    anywhere = pl.BlockSpec(memory_space=pl.ANY)
    return pl.pallas_call(
        hand_over,
        out_shape=shapes,
        in_specs=[anywhere] * 3,
        out_specs=(anywhere,) * 3,
        scratch_shapes=[pltpu.VMEM(shape.shape, jnp.float32) for shape in shapes]
        + [pltpu.SemaphoreType.DMA((3,))] * 2,
        compiler_params=pltpu.CompilerParams(vmem_limit_bytes=8 * 1024 * 1024),
        name="hand_over",
    )(*results)


def solution(mesh):
    in_specs = (
        P(None, "gy", "gx"),
        P("gy", "gx", None),
        P("gx", "gy", None),
        P("gx", "gy"),
        P("gx", "gy"),
        P(None, "gx", "gy"),
        P("gx", "gy"),
        P("gx", "gy"),
        P("gx", "gy"),
    )
    out_specs = (P("gy", "gx"), P(None, "gx", "gy"), P(None, "gx", "gy"))
    return jax.shard_map(
        per_device, mesh=mesh, in_specs=in_specs, out_specs=out_specs, check_vma=False
    )
```

profile of v0, /device:TPU:0, one launch (start us, length us, event | category | flops | bytes accessed | tf_op | source)
XLA Modules:
  0.0 41.6 jit_solution(6672496866792162156)
XLA Ops:
  0.6 39.7 %window.1 = (f32[96,128]{1,0:T(8,128)S(1)}, f32[8,128,128]{2,1,0:T(8,128)S(1)}, f32[3,128,128]{2,1,0:T(8,128)S(1)}) custom-call(bf16[4,96,128]{2,1,0:T(8,128)(2,1)} %sky_far.1, bf16[96,128,128]{2,1,0:T(8,128)(2,1)} %weights_far.1, s32[1,96]{1,0:T(1,128)} %bitcast.1, s32[1,96]{1,0:T(1,128)} %lines_far.1, s32[128,128]{1,0:T(8,128)} %sea_far.1, ...), custom_call_target="tpu_custom_call" | custom-call | tf_op jit(solution)/shard_map/window/pallas_call | solution.py:663
  40.3 1.3 %hand_over.1 = (f32[96,128]{1,0:T(8,128)}, f32[8,128,128]{2,1,0:T(8,128)}, f32[3,128,128]{2,1,0:T(8,128)}) custom-call(f32[96,128]{1,0:T(8,128)S(1)} %get-tuple-element.6.refs_0_, f32[8,128,128]{2,1,0:T(8,128)S(1)} %get-tuple-element.7.refs_1_, f32[3,128,128]{2,1,0:T(8,128)S(1)} %get-tuple-element.8.refs_2_), custom_call_target="tpu_custom_call" | custom-call | tf_op jit(solution)/shard_map/hand_over/pallas_call | solution.py:723
where the time goes:
time: 41.8 us; the launch traced here: 41.6 us
  Pallas kernels  41 us (98%)
  between operations  0.64 us (2%)
    pallas_call x1, Pallas kernels, per_device(): pl.pallas_call(window_kernel, out_shape=shapes, in_specs=[far] * 9, out_s...  39.7 us
    pallas_call x1, Pallas kernels, per_device(): pl.pallas_call(hand_over, out_shape=shapes, in_specs=[anywhere] * 3, out_...  1.27 us

commit v1 on v0

--- a/solution.py
+++ b/solution.py
@@ -38,6 +38,9 @@
 SLOTS = 8
 FLUXES = 4
 PARTS = 4
+EDGES = 16
+HEIGHT_EDGE = MARINE_STRATA
+WET_EDGE = MARINE_STRATA + 1
 
 
 def turn_lanes(values, shift):
@@ -95,7 +98,7 @@
                 copy.wait()
             return carry
 
-        lax.fori_loop(0 if dy else 1, nx, one, 0)
+        lax.fori_loop(0 if dy else 1, nx, one, 0, unroll=True)
 
 
 def as_bits(condition):
@@ -188,15 +191,19 @@
     )
 
 
-def fill_heat_edges(heat, edges):
+def fill_edges(heat, height, wet, edges):
     selector = edge_selector(8, 0, 1)
-    for k in range(MARINE_STRATA):
-        level = slice(k, k + 1)
-        edges[0, level] = heat[k, 0:1]
-        edges[1, level] = heat[k, OX - 1 : OX]
-        sides = dot(selector, heat[k].astype(jnp.bfloat16), 1, 1)
-        edges[2, level] = sides[0:1]
-        edges[3, level] = sides[1:2]
+    blank = jnp.zeros((EDGES - MARINE_STRATA, LANES), jnp.float32)
+    for end in range(4):
+        edges[end, MARINE_STRATA:EDGES] = blank
+    fields = [heat[k] for k in range(MARINE_STRATA)] + [height, wet]
+    for k, values in enumerate(fields):
+        row = slice(k, k + 1)
+        edges[0, row] = values[0:1]
+        edges[1, row] = values[OX - 1 : OX]
+        sides = dot(selector, values.astype(jnp.bfloat16), 1, 1)
+        edges[2, row] = sides[0:1]
+        edges[3, row] = sides[1:2]
 
 
 def heat_copies(edges, got, send_sem, recv_sem):
@@ -215,18 +222,19 @@
     ]
 
 
-def heat_step(heat, got, tall, shore, left_wet, right_wet, near, out):
+def heat_step(heat, got, tall, shore, near, out):
     last = lanes(OX) == LANES - 1
     first = lanes(OX) == 0
     mine = shore[8 : 8 + OX]
-    near[0] = jnp.where(last, turn_lanes(right_wet, -1), turn_lanes(mine, -1))
-    near[1] = jnp.where(first, turn_lanes(left_wet, 1), turn_lanes(mine, 1))
     sides = jnp.concatenate([got[3], got[2]], axis=0).astype(jnp.bfloat16)
+    wet = dot(sides, edge_selector(2 * EDGES, EDGES + WET_EDGE, WET_EDGE), 0, 0)
+    near[0] = jnp.where(last, wet, turn_lanes(mine, -1))
+    near[1] = jnp.where(first, wet, turn_lanes(mine, 1))
     for k in range(MARINE_STRATA):
         tall[k, 8 : 8 + OX] = heat[k]
         tall[k, 7:8] = got[0, k : k + 1]
         tall[k, 8 + OX : 9 + OX] = got[1, k : k + 1]
-        near[2 + k] = dot(sides, edge_selector(2 * MARINE_STRATA, MARINE_STRATA + k, k), 0, 0)
+        near[2 + k] = dot(sides, edge_selector(2 * EDGES, EDGES + k, k), 0, 0)
 
     step = 32
     last, first = last[:step], first[:step]
@@ -263,7 +271,7 @@
 
 
 class Exchange:
-    def __init__(self, rows, edge, packs, sides, send, recv, wrap):
+    def __init__(self, rows, edge, packs, sides, send, recv):
         x, y, up, down, right, left = neighbours()
         ny = lax.axis_size("gy")
         low, high = packs.at[0], packs.at[1]
@@ -285,17 +293,14 @@
             remote(low.at[src], from_right.at[dst], (to, left), send, recv, 3 + k)
             for k, (src, dst, to) in enumerate(moves)
         ]
-        self.wrap, self.has_right, self.has_left = wrap, y < ny - 1, y > 0
+        self.has_right, self.has_left = y < ny - 1, y > 0
 
     def guarded(self, condition, copies, action):
         def act():
             for copy in copies:
                 getattr(copy, action)()
 
-        if self.wrap:
-            act()
-        else:
-            pl.when(condition)(act)
+        pl.when(condition)(act)
 
     def start(self):
         self.guarded(self.has_right, self.right, "start")
@@ -384,6 +389,25 @@
         gain[1, here] = PRESS_GAIN * turn_lanes(two, -MARGIN)
 
 
+def height_over_wall(got, state):
+    y, ny = lax.axis_index("gy"), lax.axis_size("gy")
+    row = lax.broadcasted_iota(jnp.int32, (2 * EDGES, LANES), 0)
+    lane = lanes(2 * EDGES)
+    low = (row == EDGES + HEIGHT_EDGE) & (lane == MARGIN - 1)
+    high = (row == HEIGHT_EDGE) & (lane == LANES - MARGIN)
+    sides = jnp.concatenate([got[3], got[2]], axis=0).astype(jnp.bfloat16)
+    values = dot(sides, as_bits(low | high), 0, 0)
+    rows, lane = slice(BASE, BASE + OX), lanes(OX)
+
+    @pl.when(y == 0)
+    def _():
+        state[0, 0, rows] = jnp.where(lane == MARGIN - 1, values, state[0, 0, rows])
+
+    @pl.when(y == ny - 1)
+    def _():
+        state[0, 1, rows] = jnp.where(lane == LANES - MARGIN, values, state[0, 1, rows])
+
+
 def renew_overlap(state, reach):
     low, high = BASE - reach, BASE + OX + reach
     shift = LANES - 2 * MARGIN + 2 * OVERLAP
@@ -442,11 +466,9 @@
     for start in starts:
         for tile in range(2):
             velocity(start, tile)
-        if start > low:
-            for tile in range(2):
-                surface(start - CHUNK, tile)
-    for tile in range(2):
-        surface(high - CHUNK, tile)
+    for start in starts:
+        for tile in range(2):
+            surface(start, tile)
 
 
 def run_span(state, forces, gain, turning, raw):
@@ -464,7 +486,7 @@
             substep(reach, state, forces, gain, turning, False)
             return carry
 
-        lax.fori_loop(1 if raw and done == 0 else 0, steps, one, 0)
+        lax.fori_loop(1 if raw and done == 0 else 0, steps, one, 0, unroll=True)
         done += steps
 
 
@@ -484,20 +506,21 @@
     count = lax.axis_size("gx") * ny
     most = max(2, 2 * NB // count)
     me = lax.axis_index("gx") * ny + lax.axis_index("gy")
-    greet_all(me, count)
     part = NB // PARTS
     pieces = [pl.ds(p * part, part) for p in range(PARTS)]
     moves = [(keeper_far, keeper), (lines_far, lines), (sky_far, sky)]
-    moves += [(weights_far.at[piece], weights.at[piece]) for piece in pieces]
-    moves += [(sea_far, sea), (h_far, natural.at[0]), (u_far, natural.at[1])]
-    moves += [(v_far, natural.at[2]), (heat_far, heat)]
+    moves += [(weights_far.at[pieces[0]], weights.at[pieces[0]])]
+    moves += [(sea_far, sea), (h_far, natural.at[0]), (heat_far, heat)]
+    moves += [(weights_far.at[piece], weights.at[piece]) for piece in pieces[1:]]
+    moves += [(u_far, natural.at[1]), (v_far, natural.at[2])]
     loads = [
         pltpu.make_async_copy(src, dst, load_sem.at[k]) for k, (src, dst) in enumerate(moves)
     ]
     for load in loads:
         load.start()
+    greet_all(me, count)
     turning[...] = turning_rows()
-    clear_walls((sides2, sides3, wets_in))
+    clear_walls((sides1, sides2, sides3, wets_in))
     blank = jnp.zeros((8, LANES), jnp.float32)
     for f in range(2):
         for tile in range(2):
@@ -510,33 +533,40 @@
     for d in range(count):
         listed_out[d] = listed[d : d + 1]
     slots = as_bits(line_numbers((count * SLOTS, NB), 0) == key_row)
+    for load in loads[4:7]:
+        load.wait()
+    lat = lax.axis_index("gy") * LANES + lanes(OX)
+    inside = (lat > 0) & (lat < ny * LANES - 1)
+    shore[8 : 8 + OX] = jnp.where(inside, sea[...].astype(jnp.float32), 0.0)
+    fill_edges(heat, natural[0], shore[8 : 8 + OX], heat_edges)
+    heats = heat_copies(heat_edges, heat_got, heat_send_sem, heat_recv_sem)
     loads[2].wait()
-    regrid(sky, weights, partial, loads[3 : 3 + PARTS])
+    regrid(sky, weights, partial, [loads[3]] + loads[7 : 6 + PARTS])
     fill_send(send, stage, partial, slots, count, most)
     pl.semaphore_wait(pltpu.get_barrier_semaphore(), count - 1)
+    for copy in heats:
+        copy.start()
     peers("start", listed_out, listed_in, list_send, list_recv)
     peers("start", send, recv, a2a_send, a2a_recv)
     recv[me] = send[me]
     listed_in[me] = listed_out[me]
-    for load in loads[3 + PARTS :]:
+    for load in loads[6 + PARTS :]:
         load.wait()
-    lat = lax.axis_index("gy") * LANES + lanes(OX)
-    inside = (lat > 0) & (lat < ny * LANES - 1)
-    shore[8 : 8 + OX] = jnp.where(inside, sea[...].astype(jnp.float32), 0.0)
-    fill_heat_edges(heat, heat_edges)
-    heats = heat_copies(heat_edges, heat_got, heat_send_sem, heat_recv_sem)
-    for copy in heats:
-        copy.start()
     for f in range(3):
         fill_rows(rows1, f, natural[f])
     fill_rows(rows1, 3, shore[8 : 8 + OX])
     fill_packs(packs1, [natural[f] for f in range(3)])
     wets[0] = shore[8 : 8 + OX].astype(jnp.bfloat16)
     wets[1] = shore[8 : 8 + OX].astype(jnp.bfloat16)
-    first = Exchange(rows1, edge1, packs1, sides1, send1, recv1, True)
-    wet = Exchange(None, None, wets, wets_in, send0, recv0, False)
+    first = Exchange(rows1, edge1, packs1, sides1, send1, recv1)
+    wet = Exchange(None, None, wets, wets_in, send0, recv0)
     wet.start()
     first.start()
+    for copy in heats:
+        copy.wait()
+    shore[7:8] = heat_got[0, WET_EDGE : WET_EDGE + 1]
+    shore[8 + OX : 9 + OX] = heat_got[1, WET_EDGE : WET_EDGE + 1]
+    heat_step(heat, heat_got, tall, shore, near, heat_out)
     peers("wait", listed_out, listed_in, list_send, list_recv)
     target = read_targets(listed_in, count)
     target_turned = target.T.astype(jnp.bfloat16)
@@ -554,19 +584,13 @@
     for f in range(3):
         fill_rows(rows2, f, own[f])
     fill_packs(packs2, own)
-    second = Exchange(rows2, edge2, packs2, sides2, send2, recv2, False)
+    second = Exchange(rows2, edge2, packs2, sides2, send2, recv2)
     second.start()
     wet.wait()
     first.wait()
-    for copy in heats:
-        copy.wait()
     spread_wet(shore, edge1, wets_in, gain)
     spread_fields(natural, edge1, sides1, state, gain)
-    shore[7:8] = edge1[0, 3, MARGIN - 8 : MARGIN].astype(jnp.float32)[7:8]
-    shore[8 + OX : 9 + OX] = edge1[1, 3, 0:8].astype(jnp.float32)[0:1]
-    left_wet = wets_in[0, MARGIN : MARGIN + OX].astype(jnp.float32)
-    right_wet = wets_in[1, MARGIN : MARGIN + OX].astype(jnp.float32)
-    heat_step(heat, heat_got, tall, shore, left_wet, right_wet, near, heat_out)
+    height_over_wall(heat_got, state)
     surface = heat_out[0] + HEAT_GAIN * others[:, LANES:] * shore[8 : 8 + OX]
     heat_out[0] = surface
     band = dot(target, surface.astype(jnp.bfloat16))
@@ -580,7 +604,7 @@
         natural[f] = own_part(state, f)
         fill_rows(rows3, f, natural[f])
     fill_packs(packs3, [natural[f] for f in range(3)])
-    third = Exchange(rows3, edge3, packs3, sides3, send3, recv3, False)
+    third = Exchange(rows3, edge3, packs3, sides3, send3, recv3)
     third.start()
     peers("wait", skin_send, skin_recv, skin_send_sem, skin_recv_sem)
     slots = as_bits(line_numbers((NB, count * SLOTS), 1) == key_col)
@@ -682,8 +706,8 @@
             pltpu.VMEM((count, 1, line), full),
             pltpu.VMEM((count, SLOTS, line), half),
             pltpu.VMEM((count, SLOTS, line), half),
-            pltpu.VMEM((4, MARINE_STRATA, line), full),
-            pltpu.VMEM((4, MARINE_STRATA, line), full),
+            pltpu.VMEM((4, EDGES, line), full),
+            pltpu.VMEM((4, EDGES, line), full),
             pltpu.VMEM((MARINE_STRATA, OX + 16, line), full),
             pltpu.VMEM((2 + MARINE_STRATA, OX, line), full),
             pltpu.VMEM((OX + 16, line), full),

time: 41.8 us -> 35.7 us (0.85)
  Pallas kernels: 41 us -> 34.8 us
    pallas_call x1, Pallas kernels: 39.7 us -> 33.5 us  [per_device(): pl.pallas_call(window_kernel, out_shape=shapes, in_specs=[far] * 9, out_s...]
where the time goes in v1:
time: 35.7 us; the launch traced here: 35.6 us
  Pallas kernels  34.8 us (97%)
  between operations  0.8 us (2%)
    pallas_call x1, Pallas kernels, per_device(): pl.pallas_call(window_kernel, out_shape=shapes, in_specs=[far] * 9, out_s...  33.5 us
    pallas_call x1, Pallas kernels, per_device(): pl.pallas_call(hand_over, out_shape=shapes, in_specs=[anywhere] * 3, out_...  1.27 us

profile of v1, /device:TPU:0, one launch (start us, length us, event | category | flops | bytes accessed | tf_op | source)
XLA Modules:
  0.0 35.6 jit_solution(18136879488038455205)
XLA Ops:
  0.6 33.5 %window.1 = (f32[96,128]{1,0:T(8,128)S(1)}, f32[8,128,128]{2,1,0:T(8,128)S(1)}, f32[3,128,128]{2,1,0:T(8,128)S(1)}) custom-call(bf16[4,96,128]{2,1,0:T(8,128)(2,1)} %sky_far.1, bf16[96,128,128]{2,1,0:T(8,128)(2,1)} %weights_far.1, s32[1,96]{1,0:T(1,128)} %bitcast.1, s32[1,96]{1,0:T(1,128)} %lines_far.1, s32[128,128]{1,0:T(8,128)} %sea_far.1, ...), custom_call_target="tpu_custom_call" | custom-call | tf_op jit(solution)/shard_map/window/pallas_call | solution.py:687
  34.2 1.3 %hand_over.1 = (f32[96,128]{1,0:T(8,128)}, f32[8,128,128]{2,1,0:T(8,128)}, f32[3,128,128]{2,1,0:T(8,128)}) custom-call(f32[96,128]{1,0:T(8,128)S(1)} %get-tuple-element.6.refs_0_, f32[8,128,128]{2,1,0:T(8,128)S(1)} %get-tuple-element.7.refs_1_, f32[3,128,128]{2,1,0:T(8,128)S(1)} %get-tuple-element.8.refs_2_), custom_call_target="tpu_custom_call" | custom-call | tf_op jit(solution)/shard_map/hand_over/pallas_call | solution.py:747

commit v2 on v1

--- a/solution.py
+++ b/solution.py
@@ -60,45 +60,56 @@
     return x, y, up, down, right, left
 
 
-def peer_place(index):
-    ny = lax.axis_size("gy")
-    return lax.div(index, ny), lax.rem(index, ny)
-
-
-def greet_all(me, count):
-    barrier = pltpu.get_barrier_semaphore()
-
-    def one(k, carry):
-        place = peer_place(lax.rem(me + k, count))
-        pl.semaphore_signal(barrier, inc=1, device_id=place, device_id_type=MESH)
-        return carry
-
-    lax.fori_loop(1, count, one, 0)
-
-
-def peers(action, out, into, send_sem, recv_sem):
+def far_first(act):
     nx, ny = lax.axis_size("gx"), lax.axis_size("gy")
     x, y = lax.axis_index("gx"), lax.axis_index("gy")
-    me = x * ny + y
     for dy in sorted(range(ny), key=lambda d: abs(2 * d - ny)):
 
         def one(dx, carry, dy=dy):
-            to_x, to_y = lax.rem(x + dx, nx), lax.rem(y + dy, ny)
-            copy = pltpu.make_async_remote_copy(
-                src_ref=out.at[to_x * ny + to_y],
-                dst_ref=into.at[me],
-                send_sem=send_sem.at[dx * ny + dy],
-                recv_sem=recv_sem.at[dx * ny + dy],
-                device_id=(to_x, to_y),
-                device_id_type=MESH,
-            )
-            if action == "start":
-                copy.start()
-            else:
-                copy.wait()
+            act(lax.rem(x + dx, nx), lax.rem(y + dy, ny))
             return carry
 
         lax.fori_loop(0 if dy else 1, nx, one, 0, unroll=True)
+
+
+def greet_all():
+    barrier = pltpu.get_barrier_semaphore()
+
+    def greet(to_x, to_y):
+        pl.semaphore_signal(barrier, inc=1, device_id=(to_x, to_y), device_id_type=MESH)
+
+    far_first(greet)
+
+
+def remote(src, dst, place, send_sem, recv_sem):
+    return pltpu.make_async_remote_copy(
+        src_ref=src,
+        dst_ref=dst,
+        send_sem=send_sem,
+        recv_sem=recv_sem,
+        device_id=place,
+        device_id_type=MESH,
+    )
+
+
+class Swap:
+    def __init__(self, out, into, send_sem, recv_sem):
+        self.out, self.into, self.sems = out, into, (send_sem, recv_sem)
+
+    def start(self):
+        ny = lax.axis_size("gy")
+        me = lax.axis_index("gx") * ny + lax.axis_index("gy")
+
+        def send(to_x, to_y):
+            place = (to_x, to_y)
+            remote(self.out.at[to_x * ny + to_y], self.into.at[me], place, *self.sems).start()
+
+        far_first(send)
+
+    def wait(self):
+        x, y, up, down, right, left = neighbours()
+        others = pl.ds(0, lax.axis_size("gx") * lax.axis_size("gy") - 1)
+        remote(self.out.at[others], self.into.at[others], (up, y), *self.sems).wait()
 
 
 def as_bits(condition):
@@ -206,20 +217,19 @@
         edges[3, row] = sides[1:2]
 
 
-def heat_copies(edges, got, send_sem, recv_sem):
-    x, y, up, down, right, left = neighbours()
-    plan = ((1, 0, (up, y)), (0, 1, (down, y)), (3, 2, (x, right)), (2, 3, (x, left)))
-    return [
-        pltpu.make_async_remote_copy(
-            src_ref=edges.at[src],
-            dst_ref=got.at[dst],
-            send_sem=send_sem.at[k],
-            recv_sem=recv_sem.at[k],
-            device_id=place,
-            device_id_type=MESH,
-        )
-        for k, (src, dst, place) in enumerate(plan)
-    ]
+class EdgeSwap:
+    def __init__(self, edges, got, send_sem, recv_sem):
+        self.edges, self.got, self.sems = edges, got, (send_sem, recv_sem)
+
+    def start(self):
+        x, y, up, down, right, left = neighbours()
+        plan = ((1, 0, (up, y)), (0, 1, (down, y)), (3, 2, (x, right)), (2, 3, (x, left)))
+        for src, dst, place in plan:
+            remote(self.edges.at[src], self.got.at[dst], place, *self.sems).start()
+
+    def wait(self):
+        x, y, up, down, right, left = neighbours()
+        remote(self.edges, self.got, (up, y), *self.sems).wait()
 
 
 def heat_step(heat, got, tall, shore, near, out):
@@ -259,77 +269,55 @@
     lax.fori_loop(0, MARINE_STRATA, one, 0)
 
 
-def remote(src, dst, place, send, recv, k):
-    return pltpu.make_async_remote_copy(
-        src_ref=src,
-        dst_ref=dst,
-        send_sem=send.at[k],
-        recv_sem=recv.at[k],
-        device_id=place,
-        device_id_type=MESH,
-    )
-
-
 class Exchange:
     def __init__(self, rows, edge, packs, sides, send, recv):
+        self.rows, self.edge, self.packs, self.sides = rows, edge, packs, sides
+        self.sems = [(send.at[k], recv.at[k]) for k in range(3)]
+
+    def start_sides(self):
         x, y, up, down, right, left = neighbours()
         ny = lax.axis_size("gy")
-        low, high = packs.at[0], packs.at[1]
-        from_left, from_right = sides.at[0], sides.at[1]
         top, whole, bottom = pl.ds(OX - MARGIN, MARGIN), pl.ds(0, OX), pl.ds(0, MARGIN)
         before, middle, after = pl.ds(0, MARGIN), pl.ds(MARGIN, OX), pl.ds(MARGIN + OX, MARGIN)
         moves = ((top, before, up), (bottom, after, down), (whole, middle, x))
-        self.rows = []
-        if rows is not None:
-            self.rows = [
-                remote(rows.at[1], edge.at[0], (up, y), send, recv, 6),
-                remote(rows.at[0], edge.at[1], (down, y), send, recv, 7),
-            ]
-        self.right = [
-            remote(high.at[src], from_left.at[dst], (to, right), send, recv, k)
-            for k, (src, dst, to) in enumerate(moves)
-        ]
-        self.left = [
-            remote(low.at[src], from_right.at[dst], (to, left), send, recv, 3 + k)
-            for k, (src, dst, to) in enumerate(moves)
-        ]
-        self.has_right, self.has_left = y < ny - 1, y > 0
-
-    def guarded(self, condition, copies, action):
-        def act():
-            for copy in copies:
-                getattr(copy, action)()
-
-        pl.when(condition)(act)
-
-    def start(self):
-        self.guarded(self.has_right, self.right, "start")
-        self.guarded(self.has_left, self.left, "start")
-        for copy in self.rows:
-            copy.start()
+
+        def send(side, to_y, sems):
+            for src, dst, to_x in moves:
+                remote(
+                    self.packs.at[1 - side, :, src], self.sides.at[side, :, dst], (to_x, to_y), *sems
+                ).start()
+
+        pl.when(y < ny - 1)(lambda: send(0, right, self.sems[0]))
+        pl.when(y > 0)(lambda: send(1, left, self.sems[1]))
+
+    def start_rows(self):
+        x, y, up, down, right, left = neighbours()
+        remote(self.rows.at[1], self.edge.at[0], (up, y), *self.sems[2]).start()
+        remote(self.rows.at[0], self.edge.at[1], (down, y), *self.sems[2]).start()
 
     def wait(self):
-        for copy in self.rows:
-            copy.wait()
-        self.guarded(self.has_left, self.right, "wait_recv")
-        self.guarded(self.has_right, self.left, "wait_recv")
-        self.guarded(self.has_right, self.right, "wait_send")
-        self.guarded(self.has_left, self.left, "wait_send")
+        x, y, up, down, right, left = neighbours()
+        ny = lax.axis_size("gy")
+        remote(self.rows, self.edge, (up, y), *self.sems[2]).wait()
+        rightward = remote(self.sides.at[0], self.sides.at[0], (up, y), *self.sems[0])
+        leftward = remote(self.sides.at[1], self.sides.at[1], (up, y), *self.sems[1])
+        pl.when(y > 0)(rightward.wait_recv)
+        pl.when(y < ny - 1)(leftward.wait_recv)
+        pl.when(y < ny - 1)(rightward.wait_send)
+        pl.when(y > 0)(leftward.wait_send)
 
 
 def clear_walls(sides):
     y, ny = lax.axis_index("gy"), lax.axis_size("gy")
-    blank = jnp.zeros((FRAME, LANES), jnp.bfloat16)
-
     @pl.when(y == 0)
     def _():
         for side in sides:
-            side[0] = blank
+            side[0] = jnp.zeros(side.shape[1:], jnp.bfloat16)
 
     @pl.when(y == ny - 1)
     def _():
         for side in sides:
-            side[1] = blank
+            side[1] = jnp.zeros(side.shape[1:], jnp.bfloat16)
 
 
 def fill_rows(rows, field, values):
@@ -345,8 +333,24 @@
     high = turn_lanes(values[2], 3 * MARGIN)
     high = jnp.where(lane < 2 * MARGIN, turn_lanes(values[1], 2 * MARGIN), high)
     high = jnp.where(lane < MARGIN, turn_lanes(values[0], MARGIN), high)
-    packs[0] = low.astype(jnp.bfloat16)
-    packs[1] = high.astype(jnp.bfloat16)
+    packs[0, 0] = low.astype(jnp.bfloat16)
+    packs[1, 0] = high.astype(jnp.bfloat16)
+
+
+def fill_packs_from_tiles(packs, state):
+    lane = lanes(OX)
+    own = slice(BASE, BASE + OX)
+    low = turn_lanes(state[2, 0, own], LANES - 4 * MARGIN)
+    for f in (1, 0):
+        near = lane >= LANES - (f + 1) * MARGIN
+        low = jnp.where(near, turn_lanes(state[f, 0, own], LANES - (f + 2) * MARGIN), low)
+    shift = LANES - 2 * MARGIN
+    high = turn_lanes(state[2, 1, own], 2 * MARGIN - shift)
+    for f in (1, 0):
+        near = lane < (f + 1) * MARGIN
+        high = jnp.where(near, turn_lanes(state[f, 1, own], f * MARGIN - shift), high)
+    packs[0, 0] = low.astype(jnp.bfloat16)
+    packs[1, 0] = high.astype(jnp.bfloat16)
 
 
 def zones():
@@ -361,8 +365,8 @@
     for at, side_at, size, end in zones():
         lane = lanes(size)
         here, there = slice(at, at + size), slice(side_at, side_at + size)
-        from_left = sides[0, there].astype(jnp.float32)
-        from_right = sides[1, there].astype(jnp.float32)
+        from_left = sides[0, 0, there].astype(jnp.float32)
+        from_right = sides[1, 0, there].astype(jnp.float32)
         for f in range(3):
             centre = natural[f] if end is None else edge[end, f].astype(jnp.float32)
             left = turn_lanes(from_left, -f * MARGIN)
@@ -380,8 +384,8 @@
     for at, side_at, size, end in zones():
         lane = lanes(size)
         here, there = slice(at, at + size), slice(side_at, side_at + size)
-        from_left = sides[0, there].astype(jnp.float32)
-        from_right = sides[1, there].astype(jnp.float32)
+        from_left = sides[0, 1, there].astype(jnp.float32)
+        from_right = sides[1, 1, there].astype(jnp.float32)
         centre = shore[8 : 8 + OX] if end is None else edge[end, 3].astype(jnp.float32)
         one = jnp.where(lane >= LANES - MARGIN, from_left, centre)
         two = jnp.where(lane < MARGIN, from_right, centre)
@@ -497,10 +501,10 @@
     turning, partial, stage, send, recv, listed_out, listed_in, skin_send, skin_recv,
     heat_edges, heat_got, tall, near, shore,
     state, forces, gain,
-    rows1, edge1, packs1, sides1, wets, wets_in,
+    rows1, edge1, packs1, sides1,
     rows2, edge2, packs2, sides2, rows3, edge3, packs3, sides3,
     load_sem, list_send, list_recv, a2a_send, a2a_recv, skin_send_sem, skin_recv_sem,
-    heat_send_sem, heat_recv_sem, send0, recv0, send1, recv1, send2, recv2, send3, recv3,
+    heat_send_sem, heat_recv_sem, send1, recv1, send2, recv2, send3, recv3,
 ):
     ny = lax.axis_size("gy")
     count = lax.axis_size("gx") * ny
@@ -518,9 +522,9 @@
     ]
     for load in loads:
         load.start()
-    greet_all(me, count)
+    greet_all()
     turning[...] = turning_rows()
-    clear_walls((sides1, sides2, sides3, wets_in))
+    clear_walls((sides1, sides2, sides3))
     blank = jnp.zeros((8, LANES), jnp.float32)
     for f in range(2):
         for tile in range(2):
@@ -539,39 +543,39 @@
     inside = (lat > 0) & (lat < ny * LANES - 1)
     shore[8 : 8 + OX] = jnp.where(inside, sea[...].astype(jnp.float32), 0.0)
     fill_edges(heat, natural[0], shore[8 : 8 + OX], heat_edges)
-    heats = heat_copies(heat_edges, heat_got, heat_send_sem, heat_recv_sem)
+    heats = EdgeSwap(heat_edges, heat_got, heat_send_sem, heat_recv_sem)
+    targets = Swap(listed_out, listed_in, list_send, list_recv)
+    fluxes = Swap(send, recv, a2a_send, a2a_recv)
+    skins = Swap(skin_send, skin_recv, skin_send_sem, skin_recv_sem)
     loads[2].wait()
     regrid(sky, weights, partial, [loads[3]] + loads[7 : 6 + PARTS])
     fill_send(send, stage, partial, slots, count, most)
     pl.semaphore_wait(pltpu.get_barrier_semaphore(), count - 1)
-    for copy in heats:
-        copy.start()
-    peers("start", listed_out, listed_in, list_send, list_recv)
-    peers("start", send, recv, a2a_send, a2a_recv)
+    heats.start()
+    targets.start()
+    fluxes.start()
     recv[me] = send[me]
     listed_in[me] = listed_out[me]
     for load in loads[6 + PARTS :]:
         load.wait()
+    fill_packs(packs1, [natural[f] for f in range(3)])
+    for side in range(2):
+        packs1[side, 1] = shore[8 : 8 + OX].astype(jnp.bfloat16)
     for f in range(3):
         fill_rows(rows1, f, natural[f])
     fill_rows(rows1, 3, shore[8 : 8 + OX])
-    fill_packs(packs1, [natural[f] for f in range(3)])
-    wets[0] = shore[8 : 8 + OX].astype(jnp.bfloat16)
-    wets[1] = shore[8 : 8 + OX].astype(jnp.bfloat16)
     first = Exchange(rows1, edge1, packs1, sides1, send1, recv1)
-    wet = Exchange(None, None, wets, wets_in, send0, recv0)
-    wet.start()
-    first.start()
-    for copy in heats:
-        copy.wait()
+    first.start_sides()
+    first.start_rows()
+    heats.wait()
     shore[7:8] = heat_got[0, WET_EDGE : WET_EDGE + 1]
     shore[8 + OX : 9 + OX] = heat_got[1, WET_EDGE : WET_EDGE + 1]
     heat_step(heat, heat_got, tall, shore, near, heat_out)
-    peers("wait", listed_out, listed_in, list_send, list_recv)
+    targets.wait()
     target = read_targets(listed_in, count)
     target_turned = target.T.astype(jnp.bfloat16)
     target = target.astype(jnp.bfloat16)
-    peers("wait", send, recv, a2a_send, a2a_recv)
+    fluxes.wait()
     values = read_fluxes(recv, stage, count, most)
     stress = dot(target_turned, jnp.concatenate([values[0], values[1]], axis=1))
     others = dot(target_turned, jnp.concatenate([values[3], values[2]], axis=1))
@@ -581,32 +585,33 @@
         WIND_GAIN * stress[:, LANES:] * mask,
         FRESH_GAIN * others[:, :LANES] * mask,
     ]
+    second = Exchange(rows2, edge2, packs2, sides2, send2, recv2)
+    fill_packs(packs2, own)
+    second.start_sides()
     for f in range(3):
         fill_rows(rows2, f, own[f])
-    fill_packs(packs2, own)
-    second = Exchange(rows2, edge2, packs2, sides2, send2, recv2)
-    second.start()
-    wet.wait()
+    second.start_rows()
     first.wait()
-    spread_wet(shore, edge1, wets_in, gain)
+    spread_wet(shore, edge1, sides1, gain)
     spread_fields(natural, edge1, sides1, state, gain)
     height_over_wall(heat_got, state)
     surface = heat_out[0] + HEAT_GAIN * others[:, LANES:] * shore[8 : 8 + OX]
     heat_out[0] = surface
     band = dot(target, surface.astype(jnp.bfloat16))
     skin_send[...] = band.reshape(count, SLOTS, LANES).astype(jnp.bfloat16)
-    peers("start", skin_send, skin_recv, skin_send_sem, skin_recv_sem)
+    skins.start()
     skin_recv[me] = skin_send[me]
     second.wait()
     spread_fields(own, edge2, sides2, forces, None)
     run_span(state, forces, gain, turning, True)
+    third = Exchange(rows3, edge3, packs3, sides3, send3, recv3)
+    fill_packs_from_tiles(packs3, state)
+    third.start_sides()
     for f in range(3):
         natural[f] = own_part(state, f)
         fill_rows(rows3, f, natural[f])
-    fill_packs(packs3, [natural[f] for f in range(3)])
-    third = Exchange(rows3, edge3, packs3, sides3, send3, recv3)
-    third.start()
-    peers("wait", skin_send, skin_recv, skin_send_sem, skin_recv_sem)
+    third.start_rows()
+    skins.wait()
     slots = as_bits(line_numbers((NB, count * SLOTS), 1) == key_col)
     skin = dot(slots, skin_recv[...].reshape(count * SLOTS, LANES))
     slot8 = lax.broadcasted_iota(jnp.int32, (SLOTS, LANES), 0)
@@ -635,19 +640,10 @@
 
 
 def hand_over(*refs):
-    sources, targets = refs[:3], refs[3:6]
-    buffers, loads, stores = refs[6:9], refs[9], refs[10]
-    into = [
-        pltpu.make_async_copy(sources[k], buffers[k], loads.at[k]) for k in range(3)
-    ]
-    away = [
-        pltpu.make_async_copy(buffers[k], targets[k], stores.at[k]) for k in range(3)
-    ]
-    for copy in into:
+    sources, targets, stores = refs[:3], refs[3:6], refs[6]
+    away = [pltpu.make_async_copy(sources[k], targets[k], stores.at[k]) for k in range(3)]
+    for copy in away:
         copy.start()
-    for k in range(3):
-        into[k].wait()
-        away[k].start()
     for copy in away:
         copy.wait()
 
@@ -669,12 +665,12 @@
     half = jnp.bfloat16
     full = jnp.float32
 
-    def boxes(fields):
+    def boxes(fields, kinds):
         return [
             pltpu.VMEM((2, fields, MARGIN, line), half),
             pltpu.VMEM((2, fields, MARGIN, line), half),
-            pltpu.VMEM((2, OX, line), half),
-            pltpu.VMEM((2, FRAME, line), half),
+            pltpu.VMEM((2, kinds, OX, line), half),
+            pltpu.VMEM((2, kinds, FRAME, line), half),
         ]
 
     inside = pl.BlockSpec(memory_space=pltpu.VMEM)
@@ -715,14 +711,12 @@
             pltpu.VMEM((3, 2, TALL, line), full),
             pltpu.VMEM((2, TALL, line), full),
         ]
-        + boxes(4)
-        + [pltpu.VMEM((2, OX, line), half), pltpu.VMEM((2, FRAME, line), half)]
-        + boxes(3)
-        + boxes(3)
+        + boxes(4, 2)
+        + boxes(3, 1)
+        + boxes(3, 1)
         + [pltpu.SemaphoreType.DMA((3 + PARTS + 5,))]
-        + [pltpu.SemaphoreType.DMA((count,))] * 6
-        + [pltpu.SemaphoreType.DMA((4,))] * 2
-        + [pltpu.SemaphoreType.DMA((8,))] * 8,
+        + [pltpu.SemaphoreType.DMA] * 8
+        + [pltpu.SemaphoreType.DMA((3,))] * 6,
         compiler_params=pltpu.CompilerParams(
             collective_id=0, has_side_effects=True, vmem_limit_bytes=24 * 1024 * 1024
         ),
@@ -749,8 +743,7 @@
         out_shape=shapes,
         in_specs=[anywhere] * 3,
         out_specs=(anywhere,) * 3,
-        scratch_shapes=[pltpu.VMEM(shape.shape, jnp.float32) for shape in shapes]
-        + [pltpu.SemaphoreType.DMA((3,))] * 2,
+        scratch_shapes=[pltpu.SemaphoreType.DMA((3,))],
         compiler_params=pltpu.CompilerParams(vmem_limit_bytes=8 * 1024 * 1024),
         name="hand_over",
     )(*results)

time: 35.7 us -> 33.3 us (0.933)
  Pallas kernels: 34.8 us -> 32.4 us
    pallas_call x1, Pallas kernels: 33.5 us -> 31.5 us  [per_device(): pl.pallas_call(window_kernel, out_shape=shapes, in_specs=[far] * 9, out_s...]
    pallas_call x1, Pallas kernels: 1.27 us -> 0.89 us  [per_device(): pl.pallas_call(hand_over, out_shape=shapes, in_specs=[anywhere] * 3, out_...]
where the time goes in v2:
time: 33.3 us; the launch traced here: 33.2 us
  Pallas kernels  32.4 us (97%)
  between operations  0.8 us (2%)
    pallas_call x1, Pallas kernels, per_device(): pl.pallas_call(window_kernel, out_shape=shapes, in_specs=[far] * 9, out_s...  31.5 us
    pallas_call x1, Pallas kernels, per_device(): pl.pallas_call(hand_over, out_shape=shapes, in_specs=[anywhere] * 3, out_...  0.89 us

profile of v2, /device:TPU:0, one launch (start us, length us, event | category | flops | bytes accessed | tf_op | source)
XLA Modules:
  0.0 33.2 jit_solution(9444194235684491839)
XLA Ops:
  0.6 31.5 %window.1 = (f32[96,128]{1,0:T(8,128)S(1)}, f32[8,128,128]{2,1,0:T(8,128)S(1)}, f32[3,128,128]{2,1,0:T(8,128)S(1)}) custom-call(bf16[4,96,128]{2,1,0:T(8,128)(2,1)} %sky_far.1, bf16[96,128,128]{2,1,0:T(8,128)(2,1)} %weights_far.1, s32[1,96]{1,0:T(1,128)} %bitcast.1, s32[1,96]{1,0:T(1,128)} %lines_far.1, s32[128,128]{1,0:T(8,128)} %sea_far.1, ...), custom_call_target="tpu_custom_call" | custom-call | tf_op jit(solution)/shard_map/window/pallas_call | solution.py:683
  32.1 0.9 %hand_over.1 = (f32[96,128]{1,0:T(8,128)}, f32[8,128,128]{2,1,0:T(8,128)}, f32[3,128,128]{2,1,0:T(8,128)}) custom-call(f32[96,128]{1,0:T(8,128)S(1)} %get-tuple-element.6.refs_0_, f32[8,128,128]{2,1,0:T(8,128)S(1)} %get-tuple-element.7.refs_1_, f32[3,128,128]{2,1,0:T(8,128)S(1)} %get-tuple-element.8.refs_2_), custom_call_target="tpu_custom_call" | custom-call | tf_op jit(solution)/shard_map/hand_over/pallas_call | solution.py:741

commit v3 on v2

--- a/solution.py
+++ b/solution.py
@@ -37,6 +37,7 @@
 CHUNK = 16
 SLOTS = 8
 FLUXES = 4
+URGENT = 3
 PARTS = 4
 EDGES = 16
 HEIGHT_EDGE = MARINE_STRATA
@@ -93,8 +94,9 @@
 
 
 class Swap:
-    def __init__(self, out, into, send_sem, recv_sem):
+    def __init__(self, out, into, send_sem, recv_sem, rows):
         self.out, self.into, self.sems = out, into, (send_sem, recv_sem)
+        self.rows = pl.ds(0, rows)
 
     def start(self):
         ny = lax.axis_size("gy")
@@ -102,14 +104,16 @@
 
         def send(to_x, to_y):
             place = (to_x, to_y)
-            remote(self.out.at[to_x * ny + to_y], self.into.at[me], place, *self.sems).start()
+            src, dst = self.out.at[to_x * ny + to_y, self.rows], self.into.at[me, self.rows]
+            remote(src, dst, place, *self.sems).start()
 
         far_first(send)
 
     def wait(self):
         x, y, up, down, right, left = neighbours()
         others = pl.ds(0, lax.axis_size("gx") * lax.axis_size("gy") - 1)
-        remote(self.out.at[others], self.into.at[others], (up, y), *self.sems).wait()
+        src, dst = self.out.at[others, self.rows], self.into.at[others, self.rows]
+        remote(src, dst, (up, y), *self.sems).wait()
 
 
 def as_bits(condition):
@@ -156,20 +160,19 @@
         partial[:, rows, :] = total.reshape(FLUXES, SLOTS, LANES)
 
 
-def fill_send(send, stage, partial, slots, count, most):
+def fill_send(send, heat_send, stage, partial, slots, count, most):
     rows = FLUXES * most
     pairs = []
-    for f in range(0, FLUXES, 2):
-        both = jnp.concatenate([partial[f], partial[f + 1]], axis=1).astype(jnp.bfloat16)
+    for f, g in ((0, 1), (3, 2)):
+        both = jnp.concatenate([partial[f], partial[g]], axis=1).astype(jnp.bfloat16)
         pairs.append(dot(slots, both))
+    sources = [pairs[0][:, :LANES], pairs[0][:, LANES:], pairs[1][:, :LANES]]
     for d in range(count):
-        for f in range(FLUXES):
-            at = d * rows + f * most
-            from_lane = (f % 2) * LANES
-            stage[at : at + SLOTS] = pairs[f // 2][
-                d * SLOTS : (d + 1) * SLOTS, from_lane : from_lane + LANES
-            ]
+        for k, source in enumerate(sources):
+            at = d * rows + k * most
+            stage[at : at + SLOTS] = source[d * SLOTS : (d + 1) * SLOTS]
     send[...] = stage[0 : count * rows].reshape(count, rows, LANES).astype(jnp.bfloat16)
+    heat_send[...] = pairs[1][:, LANES:].reshape(count, SLOTS, LANES).astype(jnp.bfloat16)
 
 
 def read_targets(listed_in, count):
@@ -183,12 +186,18 @@
     return jnp.concatenate(tiles, axis=0)
 
 
+def received(values, rows):
+    row = lax.broadcasted_iota(jnp.int32, values.shape, 1)
+    flat = (values.shape[0] * values.shape[1], LANES)
+    return jnp.where(row < rows, values.astype(jnp.float32), 0.0).reshape(flat)
+
+
 def read_fluxes(recv, stage, count, most):
     rows = FLUXES * most
-    stage[0 : count * rows] = recv[...].astype(jnp.float32).reshape(count * rows, LANES)
+    stage[0 : count * rows] = received(recv[...], URGENT * most)
     values = []
-    for f in range(FLUXES):
-        starts = [s * rows + f * most for s in range(count)]
+    for k in range(URGENT):
+        starts = [s * rows + k * most for s in range(count)]
         tiles = [stage[at : at + SLOTS] for at in starts]
         values.append(jnp.concatenate(tiles, axis=0).astype(jnp.bfloat16))
     return values
@@ -353,6 +362,14 @@
     packs[1, 0] = high.astype(jnp.bfloat16)
 
 
+def fill_rows_from_tiles(rows, field, state):
+    for end, start in enumerate((BASE, BASE + OX - MARGIN)):
+        here = slice(start, start + MARGIN)
+        one = turn_lanes(state[field, 0, here], -MARGIN)
+        two = turn_lanes(state[field, 1, here], MARGIN)
+        rows[end, field] = jnp.where(lanes(MARGIN) < HALF, one, two).astype(jnp.bfloat16)
+
+
 def zones():
     return (
         (BASE - MARGIN, 0, MARGIN, 0),
@@ -361,18 +378,27 @@
     )
 
 
-def spread_fields(natural, edge, sides, wide, mask):
+def place_own(natural, wide):
+    here = slice(BASE, BASE + OX)
+    for f in range(3):
+        wide[f, 0, here] = turn_lanes(natural[f], MARGIN)
+        wide[f, 1, here] = turn_lanes(natural[f], -MARGIN)
+
+
+def spread_fields(edge, sides, wide, mask):
     for at, side_at, size, end in zones():
         lane = lanes(size)
         here, there = slice(at, at + size), slice(side_at, side_at + size)
         from_left = sides[0, 0, there].astype(jnp.float32)
         from_right = sides[1, 0, there].astype(jnp.float32)
         for f in range(3):
-            centre = natural[f] if end is None else edge[end, f].astype(jnp.float32)
-            left = turn_lanes(from_left, -f * MARGIN)
-            right = turn_lanes(from_right, f * MARGIN)
-            one = jnp.where(lane < MARGIN, left, turn_lanes(centre, MARGIN))
-            two = jnp.where(lane >= LANES - MARGIN, right, turn_lanes(centre, -MARGIN))
+            if end is None:
+                one, two = wide[f, 0, here], wide[f, 1, here]
+            else:
+                centre = edge[end, f].astype(jnp.float32)
+                one, two = turn_lanes(centre, MARGIN), turn_lanes(centre, -MARGIN)
+            one = jnp.where(lane < MARGIN, turn_lanes(from_left, -f * MARGIN), one)
+            two = jnp.where(lane >= LANES - MARGIN, turn_lanes(from_right, f * MARGIN), two)
             if mask is not None and f > 0:
                 one = jnp.where(mask[0, here] > 0, one, 0.0)
                 two = jnp.where(mask[1, here] > 0, two, 0.0)
@@ -498,12 +524,12 @@
     sky_far, weights_far, keeper_far, lines_far, sea_far, heat_far, h_far, u_far, v_far,
     back, heat_out, out,
     sky, weights, keeper, lines, sea, heat, natural,
-    turning, partial, stage, send, recv, listed_out, listed_in, skin_send, skin_recv,
+    turning, partial, stage, send, recv, warm_send, warm_recv, listed_out, listed_in, skin_send, skin_recv,
     heat_edges, heat_got, tall, near, shore,
     state, forces, gain,
     rows1, edge1, packs1, sides1,
     rows2, edge2, packs2, sides2, rows3, edge3, packs3, sides3,
-    load_sem, list_send, list_recv, a2a_send, a2a_recv, skin_send_sem, skin_recv_sem,
+    load_sem, list_send, list_recv, a2a_send, a2a_recv, warm_send_sem, warm_recv_sem, skin_send_sem, skin_recv_sem,
     heat_send_sem, heat_recv_sem, send1, recv1, send2, recv2, send3, recv3,
 ):
     ny = lax.axis_size("gy")
@@ -513,9 +539,8 @@
     part = NB // PARTS
     pieces = [pl.ds(p * part, part) for p in range(PARTS)]
     moves = [(keeper_far, keeper), (lines_far, lines), (sky_far, sky)]
-    moves += [(weights_far.at[pieces[0]], weights.at[pieces[0]])]
+    moves += [(weights_far.at[piece], weights.at[piece]) for piece in pieces]
     moves += [(sea_far, sea), (h_far, natural.at[0]), (heat_far, heat)]
-    moves += [(weights_far.at[piece], weights.at[piece]) for piece in pieces[1:]]
     moves += [(u_far, natural.at[1]), (v_far, natural.at[2])]
     loads = [
         pltpu.make_async_copy(src, dst, load_sem.at[k]) for k, (src, dst) in enumerate(moves)
@@ -537,25 +562,27 @@
     for d in range(count):
         listed_out[d] = listed[d : d + 1]
     slots = as_bits(line_numbers((count * SLOTS, NB), 0) == key_row)
-    for load in loads[4:7]:
+    loads[2].wait()
+    regrid(sky, weights, partial, loads[3 : 3 + PARTS])
+    fill_send(send, warm_send, stage, partial, slots, count, most)
+    for load in loads[3 + PARTS : 6 + PARTS]:
         load.wait()
     lat = lax.axis_index("gy") * LANES + lanes(OX)
     inside = (lat > 0) & (lat < ny * LANES - 1)
     shore[8 : 8 + OX] = jnp.where(inside, sea[...].astype(jnp.float32), 0.0)
     fill_edges(heat, natural[0], shore[8 : 8 + OX], heat_edges)
     heats = EdgeSwap(heat_edges, heat_got, heat_send_sem, heat_recv_sem)
-    targets = Swap(listed_out, listed_in, list_send, list_recv)
-    fluxes = Swap(send, recv, a2a_send, a2a_recv)
-    skins = Swap(skin_send, skin_recv, skin_send_sem, skin_recv_sem)
-    loads[2].wait()
-    regrid(sky, weights, partial, [loads[3]] + loads[7 : 6 + PARTS])
-    fill_send(send, stage, partial, slots, count, most)
+    targets = Swap(listed_out, listed_in, list_send, list_recv, 1)
+    fluxes = Swap(send, recv, a2a_send, a2a_recv, URGENT * most)
+    warmth = Swap(warm_send, warm_recv, warm_send_sem, warm_recv_sem, most)
+    skins = Swap(skin_send, skin_recv, skin_send_sem, skin_recv_sem, SLOTS)
     pl.semaphore_wait(pltpu.get_barrier_semaphore(), count - 1)
     heats.start()
     targets.start()
     fluxes.start()
     recv[me] = send[me]
     listed_in[me] = listed_out[me]
+    warm_recv[me] = warm_send[me]
     for load in loads[6 + PARTS :]:
         load.wait()
     fill_packs(packs1, [natural[f] for f in range(3)])
@@ -567,6 +594,8 @@
     first = Exchange(rows1, edge1, packs1, sides1, send1, recv1)
     first.start_sides()
     first.start_rows()
+    warmth.start()
+    place_own(natural, state)
     heats.wait()
     shore[7:8] = heat_got[0, WET_EDGE : WET_EDGE + 1]
     shore[8 + OX : 9 + OX] = heat_got[1, WET_EDGE : WET_EDGE + 1]
@@ -578,12 +607,12 @@
     fluxes.wait()
     values = read_fluxes(recv, stage, count, most)
     stress = dot(target_turned, jnp.concatenate([values[0], values[1]], axis=1))
-    others = dot(target_turned, jnp.concatenate([values[3], values[2]], axis=1))
+    fresh = dot(target_turned, values[2])
     mask = shore[8 : 8 + OX]
     own = [
         WIND_GAIN * stress[:, :LANES] * mask,
         WIND_GAIN * stress[:, LANES:] * mask,
-        FRESH_GAIN * others[:, :LANES] * mask,
+        FRESH_GAIN * fresh * mask,
     ]
     second = Exchange(rows2, edge2, packs2, sides2, send2, recv2)
     fill_packs(packs2, own)
@@ -591,26 +620,29 @@
     for f in range(3):
         fill_rows(rows2, f, own[f])
     second.start_rows()
+    place_own(own, forces)
     first.wait()
     spread_wet(shore, edge1, sides1, gain)
-    spread_fields(natural, edge1, sides1, state, gain)
+    spread_fields(edge1, sides1, state, gain)
     height_over_wall(heat_got, state)
-    surface = heat_out[0] + HEAT_GAIN * others[:, LANES:] * shore[8 : 8 + OX]
+    warmth.wait()
+    heat_flux = dot(target_turned, received(warm_recv[...], most).astype(jnp.bfloat16))
+    surface = heat_out[0] + HEAT_GAIN * heat_flux * shore[8 : 8 + OX]
     heat_out[0] = surface
     band = dot(target, surface.astype(jnp.bfloat16))
     skin_send[...] = band.reshape(count, SLOTS, LANES).astype(jnp.bfloat16)
     skins.start()
     skin_recv[me] = skin_send[me]
     second.wait()
-    spread_fields(own, edge2, sides2, forces, None)
+    spread_fields(edge2, sides2, forces, None)
     run_span(state, forces, gain, turning, True)
     third = Exchange(rows3, edge3, packs3, sides3, send3, recv3)
     fill_packs_from_tiles(packs3, state)
     third.start_sides()
     for f in range(3):
-        natural[f] = own_part(state, f)
-        fill_rows(rows3, f, natural[f])
+        fill_rows_from_tiles(rows3, f, state)
     third.start_rows()
+    renew_overlap(state, 0)
     skins.wait()
     slots = as_bits(line_numbers((NB, count * SLOTS), 1) == key_col)
     skin = dot(slots, skin_recv[...].reshape(count * SLOTS, LANES))
@@ -623,7 +655,7 @@
             total = jnp.where(slot8 == n, dot(lines_skin, weights[g * SLOTS + n], 1, 1), total)
         back[rows] = total
     third.wait()
-    spread_fields(natural, edge3, sides3, state, None)
+    spread_fields(edge3, sides3, state, None)
     run_span(state, forces, gain, turning, False)
     for f in range(3):
         out[f] = own_part(state, f)
@@ -698,6 +730,8 @@
             pltpu.VMEM((count * FLUXES * most + SLOTS, line), full),
             pltpu.VMEM((count, FLUXES * most, line), half),
             pltpu.VMEM((count, FLUXES * most, line), half),
+            pltpu.VMEM((count, SLOTS, line), half),
+            pltpu.VMEM((count, SLOTS, line), half),
             pltpu.VMEM((count, 1, line), full),
             pltpu.VMEM((count, 1, line), full),
             pltpu.VMEM((count, SLOTS, line), half),
@@ -715,7 +749,7 @@
         + boxes(3, 1)
         + boxes(3, 1)
         + [pltpu.SemaphoreType.DMA((3 + PARTS + 5,))]
-        + [pltpu.SemaphoreType.DMA] * 8
+        + [pltpu.SemaphoreType.DMA] * 10
         + [pltpu.SemaphoreType.DMA((3,))] * 6,
         compiler_params=pltpu.CompilerParams(
             collective_id=0, has_side_effects=True, vmem_limit_bytes=24 * 1024 * 1024

time: 33.3 us -> 31 us (0.931)
  Pallas kernels: 32.4 us -> 30 us
    pallas_call x1, Pallas kernels: 31.5 us -> 29.1 us  [per_device(): pl.pallas_call(window_kernel, out_shape=shapes, in_specs=[far] * 9, out_s...]
where the time goes in v3:
time: 31 us; the launch traced here: 30.8 us
  Pallas kernels  30 us (97%)
  between operations  0.8 us (3%)
    pallas_call x1, Pallas kernels, per_device(): pl.pallas_call(window_kernel, out_shape=shapes, in_specs=[far] * 9, out_s...  29.1 us
    pallas_call x1, Pallas kernels, per_device(): pl.pallas_call(hand_over, out_shape=shapes, in_specs=[anywhere] * 3, out_...  0.89 us

profile of v3, /device:TPU:0, one launch (start us, length us, event | category | flops | bytes accessed | tf_op | source)
XLA Modules:
  0.0 30.8 jit_solution(13962996342390974849)
XLA Ops:
  0.6 29.1 %window.1 = (f32[96,128]{1,0:T(8,128)S(1)}, f32[8,128,128]{2,1,0:T(8,128)S(1)}, f32[3,128,128]{2,1,0:T(8,128)S(1)}) custom-call(bf16[4,96,128]{2,1,0:T(8,128)(2,1)} %sky_far.1, bf16[96,128,128]{2,1,0:T(8,128)(2,1)} %weights_far.1, s32[1,96]{1,0:T(1,128)} %bitcast.1, s32[1,96]{1,0:T(1,128)} %lines_far.1, s32[128,128]{1,0:T(8,128)} %sea_far.1, ...), custom_call_target="tpu_custom_call" | custom-call | tf_op jit(solution)/shard_map/window/pallas_call | solution.py:715
  29.8 0.9 %hand_over.1 = (f32[96,128]{1,0:T(8,128)}, f32[8,128,128]{2,1,0:T(8,128)}, f32[3,128,128]{2,1,0:T(8,128)}) custom-call(f32[96,128]{1,0:T(8,128)S(1)} %get-tuple-element.6.refs_0_, f32[8,128,128]{2,1,0:T(8,128)S(1)} %get-tuple-element.7.refs_1_, f32[3,128,128]{2,1,0:T(8,128)S(1)} %get-tuple-element.8.refs_2_), custom_call_target="tpu_custom_call" | custom-call | tf_op jit(solution)/shard_map/hand_over/pallas_call | solution.py:775
